TPU v7x, 32 devices: a whole 2x2x4 slice. The times are simulated.
32 devices in a mesh: groups: 2 (over y), expert: 4 (over z), tensor: 4 (over x, core).
Axes of the slice: x: 2, y: 2, z: 4, core: 2. Of those that a mesh axis runs over, the one named last changes fastest.
Arguments:
- tokens: bfloat16 [2, 64, 3072], P(None, ('groups', 'expert'), 'tensor'), parts along dimension 1, may hold values from -60 to 60
- route_ids: int32 [2, 2, 64, 2], P(None, None, ('groups', 'expert')), parts along dimension 2, may hold values from 0 to 3, all different within a row; in each aligned block of 8 rows (0 to 7, 8 to 15, ..., all dimensions but the last counted through in order) at most 6 rows name the same one
- route_gates: float32 [2, 2, 64, 2], P(None, None, ('groups', 'expert')), parts along dimension 2, may hold values from 0.05 to 1
- norm_gain: float32 [2, 3072], P(None, 'tensor'), may hold values from 0.1 to 1.9
- gate_weights: bfloat16 [2, 3072, 32768], P(None, 'tensor', 'expert'), may hold values from -0.109375 to 0.109375
- up_weights: bfloat16 [2, 3072, 32768], P(None, 'tensor', 'expert'), may hold values from -0.109375 to 0.109375
- down_weights: bfloat16 [2, 32768, 3072], P(None, 'expert', 'tensor'), may hold values from -0.0625 to 0.0625
Outputs:
- layer_out: bfloat16 [2, 64, 3072], P(None, ('groups', 'expert'), 'tensor'), parts along dimension 1
There are 2 independent parts, one for each index of `groups`. A program takes and returns all parts, laid end to end along the dimension named above; an argument that names none is the same for every part. Nothing has to cross between parts.
Inputs may be any that keep to these rules, and one draw needn't show every extreme that they name: `route_ids`: in each layer and micro-batch, the 8 tokens of one expert rank name one expert at most 6 times; in some of these blocks one expert exactly 6 times. A token's two ids differ.
All inputs are finite; a program needn't handle non-finite values.
Results may differ from a plain program's by a relative error of at most 0.0085.
Values may be sent and summed in bfloat16 or wider, within the bound.
A program may use at most 128 MiB of HBM per device.

v0:
```python
import jax
import jax.numpy as jnp
from jax import lax
from jax.sharding import PartitionSpec as P

D = 3072
EXPERTS = 4


def spread_rows(normed, route_ids, expert_count, capacity):
    micro_count, token_count, row_width = normed.shape
    flat_ids = route_ids.reshape(micro_count, 2 * token_count)
    one_hot = (flat_ids[:, :, None] == jnp.arange(expert_count, dtype=jnp.int32)).astype(jnp.int32)
    earlier = jnp.cumsum(one_hot, axis=1) - one_hot
    position = jnp.sum(earlier * one_hot, axis=2)
    batch_index = jnp.arange(micro_count, dtype=jnp.int32)[:, None]
    slot_index = ((flat_ids * micro_count + batch_index) * capacity + position).reshape(-1)
    route_rows = jnp.repeat(normed, 2, axis=1).reshape(2 * micro_count * token_count, row_width)
    outgoing = (
        jnp.zeros((expert_count * micro_count * capacity, row_width), jnp.bfloat16)
        .at[slot_index]
        .set(route_rows)
    )
    return (outgoing.reshape(expert_count, micro_count * capacity, row_width), slot_index)


def make_expert(gate_matrix, up_matrix, down_weight, arrived):
    senders, item_count, row_width = arrived.shape
    inputs = arrived.reshape(senders * item_count, row_width)
    gate_part = jnp.dot(inputs, gate_matrix, preferred_element_type=jnp.float32)
    up_part = jnp.dot(inputs, up_matrix, preferred_element_type=jnp.float32)
    gate_share, up_share = (
        lax.psum_scatter(
            gate_part.astype(jnp.bfloat16), "tensor", scatter_dimension=1, tiled=True
        ).astype(jnp.float32),
        lax.psum_scatter(
            up_part.astype(jnp.bfloat16), "tensor", scatter_dimension=1, tiled=True
        ).astype(jnp.float32),
    )
    hidden = (jax.nn.silu(gate_share) * up_share).astype(jnp.bfloat16)
    result = jnp.dot(
        lax.all_gather(hidden, "tensor", axis=1, tiled=True),
        down_weight,
        preferred_element_type=jnp.float32,
    )
    outgoing = result.astype(jnp.bfloat16).reshape(senders, item_count, row_width)
    return lax.all_to_all(outgoing, "expert", split_axis=0, concat_axis=0, tiled=True)


def run_layer(current, route_ids, route_gates, gain_row, gate_matrix, up_matrix, down_weight):
    values = current.astype(jnp.float32)
    squares = lax.psum(jnp.sum(values * values, axis=2), "tensor")
    normed = (values * lax.rsqrt(squares / D + 1e-05)[:, :, None] * gain_row).astype(jnp.bfloat16)
    rank_count = lax.axis_size("expert")
    sharing = rank_count // EXPERTS
    micro_count, token_count, row_width = current.shape
    capacity = 3 * token_count // 4
    outgoing, slot_index = spread_rows(normed, route_ids, EXPERTS, capacity)
    sending = jnp.repeat(outgoing, sharing, axis=0)
    returned = make_expert(
        gate_matrix,
        up_matrix,
        down_weight,
        lax.all_to_all(sending, "expert", split_axis=0, concat_axis=0, tiled=True),
    )
    summed = jnp.sum(
        returned.astype(jnp.float32).reshape(EXPERTS, sharing, micro_count * capacity, row_width),
        axis=1,
    )
    picked = summed.reshape(-1, row_width)[slot_index].reshape(
        micro_count, token_count, 2, row_width
    )
    mixture = jnp.sum(picked * route_gates[:, :, :, None], axis=2)
    return (values + mixture).astype(jnp.bfloat16)


def shards(tokens, route_ids, route_gates, norm_gain, gate_weights, up_weights, down_weights):
    layer_count = route_ids.shape[0]
    micro_total = tokens.shape[0]
    current = tokens
    for layer_index in range(layer_count):
        current = run_layer(
            current,
            route_ids[layer_index, 0:micro_total],
            route_gates[layer_index, 0:micro_total],
            norm_gain[layer_index],
            gate_weights[layer_index],
            up_weights[layer_index],
            down_weights[layer_index],
        )
    return current


def solution(mesh):
    in_specs = (
        P(None, ("groups", "expert"), "tensor"),
        P(None, None, ("groups", "expert"), None),
        P(None, None, ("groups", "expert"), None),
        P(None, "tensor"),
        P(None, "tensor", "expert"),
        P(None, "tensor", "expert"),
        P(None, "expert", "tensor"),
    )
    out_specs = P(None, ("groups", "expert"), "tensor")
    return jax.shard_map(shards, mesh=mesh, in_specs=in_specs, out_specs=out_specs, check_vma=False)
```

profile of v0, /device:TPU:0, one launch (start us, length us, event | category | flops | bytes accessed | tf_op | source)
XLA Modules:
  0.0 219.3 jit_solution(12538534837442581928)
XLA Ops:
  6.5 0.7 broadcast_multiply_fusion.1
  8.8 0.8 slice_reduce_fusion
  9.6 0.8 fusion.46
  10.4 8.3 %psum.14 = f32[2,8]{1,0:T(2,128)S(1)} all-reduce(f32[2,8]{1,0:T(2,128)S(1)} %fusion.46), channel_id=1, replica_groups=mesh['groups'=2,'expert'=4,'tensor'=4] {'tensor'}, use_global_device_ids=true, to_apply=%region_3.4 | all-reduce | flops 16 | bytes 128 | tf_op jit(solution)/shard_map/psum | solution.py:52
  18.8 0.8 fusion.48
  19.7 0.7 scatter_custom_fusion
  20.4 10.5 %all_to_all.20 = bf16[4,12,768]{2,1,0:T(8,128)(2,1)S(1)} all-to-all(bf16[4,12,768]{2,1,0:T(8,128)(2,1)S(1)} %reshape_broadcast_in_dim_reshape.6), channel_id=1, replica_groups=mesh['groups'=2,'expert'=4,'tensor'=4] {'expert'}, dimensions={0} | all-to-all | bytes 147456 | tf_op jit(solution)/shard_map/all_to_all | solution.py:64
  31.0 7.8 %fusion.18 = bf16[48,8192]{1,0:T(8,128)(2,1)} fusion(bf16[48,768]{1,0:T(8,128)(2,1)S(1)} %reshape.142, bf16[2,768,8192]{2,1,0:T(8,128)(2,1)} %param.11), kind=kOutput, calls=%fused_computation.22 | convolution fusion | flops 604372992 | bytes 13443072 | tf_op jit(solution)/shard_map/dot_general | solution.py:30
  38.9 8.0 %fusion.21 = bf16[48,8192]{1,0:T(8,128)(2,1)} fusion(bf16[48,768]{1,0:T(8,128)(2,1)S(1)} %reshape.142, bf16[2,768,8192]{2,1,0:T(8,128)(2,1)} %param.12), kind=kOutput, calls=%fused_computation.23 | convolution fusion | flops 604372992 | bytes 13443072 | tf_op jit(solution)/shard_map/dot_general | solution.py:31
  46.9 13.0 %reduce-scatter.5.cloned.1.call-done = bf16[48,2048]{1,0:T(8,128)(2,1)} async-done(((bf16[48,8192]{1,0:T(8,128)(2,1)}), bf16[48,2048]{1,0:T(8,128)(2,1)}) %reduce-scatter.5.cloned.1.call-update) | async-done | bytes 196624 | tf_op jit(solution)/shard_map/reduce_scatter | solution.py:33
  59.9 25.8 %reduce-scatter.7.cloned.1.call-done = bf16[48,2048]{1,0:T(8,128)(2,1)} async-done(((bf16[48,8192]{1,0:T(8,128)(2,1)}), bf16[48,2048]{1,0:T(8,128)(2,1)}) %reduce-scatter.7.cloned.1.call-update) | async-done | bytes 196624 | tf_op jit(solution)/shard_map/reduce_scatter | solution.py:36
  85.7 1.1 fusion.45
  86.9 8.1 %all_gather.6 = bf16[48,8192]{1,0:T(8,128)(2,1)S(1)} all-gather(bf16[48,2048]{1,0:T(8,128)(2,1)S(1)} %fusion.45), channel_id=1, replica_groups=mesh['groups'=2,'expert'=4,'tensor'=4] {'tensor'}, dimensions={1}, use_global_device_ids=true | all-gather | bytes 983040 | tf_op jit(solution)/shard_map/all_gather | solution.py:42
  94.9 6.8 %fusion.30 = bf16[48,768]{1,0:T(8,128)(2,1)S(1)} fusion(bf16[48,8192]{1,0:T(8,128)(2,1)S(1)} %all_gather.6, bf16[2,8192,768]{2,1,0:T(8,128)(2,1)} %param.13), kind=kOutput, calls=%fused_computation.26 | convolution fusion | flops 604016640 | bytes 13443072 | tf_op jit(solution)/shard_map/dot_general | solution.py:41
  101.7 0.6 reshape.143
  102.4 4.6 %all-to-all-start.1 = ((bf16[4,12,768]{2,1,0:T(8,128)(2,1)}), bf16[4,12,768]{2,1,0:T(8,128)(2,1)S(1)}, u32[]{:S(2)}, u32[]{:S(2)}) async-start(bf16[4,12,768]{2,1,0:T(8,128)(2,1)} %reshape.143), calls=%async_computation.3 | async-start | bytes 196608 | tf_op jit(solution)/shard_map/all_to_all | solution.py:47
  107.0 6.0 %all-to-all-done.1 = bf16[4,12,768]{2,1,0:T(8,128)(2,1)S(1)} async-done(((bf16[4,12,768]{2,1,0:T(8,128)(2,1)}), bf16[4,12,768]{2,1,0:T(8,128)(2,1)S(1)}, u32[]{:S(2)}, u32[]{:S(2)}) %all-to-all-start.1) | async-done | bytes 73760 | tf_op jit(solution)/shard_map/all_to_all | solution.py:47
  114.0 5.6 %psum.15 = f32[2,8]{1,0:T(2,128)S(1)} all-reduce(f32[2,8]{1,0:T(2,128)S(1)} %get-tuple-element.7), channel_id=1, replica_groups=mesh['groups'=2,'expert'=4,'tensor'=4] {'tensor'}, use_global_device_ids=true, to_apply=%region_11.12 | all-reduce | flops 16 | bytes 128 | tf_op jit(solution)/shard_map/psum | solution.py:52
  119.7 0.7 scatter_custom_fusion.1
  120.5 8.5 %all_to_all.21 = bf16[4,12,768]{2,1,0:T(8,128)(2,1)S(1)} all-to-all(bf16[4,12,768]{2,1,0:T(8,128)(2,1)S(1)} %reshape_broadcast_in_dim_reshape.7), channel_id=1, replica_groups=mesh['groups'=2,'expert'=4,'tensor'=4] {'expert'}, dimensions={0} | all-to-all | bytes 147456 | tf_op jit(solution)/shard_map/all_to_all | solution.py:64
  129.0 7.8 %fusion.27 = bf16[48,8192]{1,0:T(8,128)(2,1)} fusion(bf16[48,768]{1,0:T(8,128)(2,1)S(1)} %reshape.147, bf16[2,768,8192]{2,1,0:T(8,128)(2,1)} %param.12), kind=kOutput, calls=%fused_computation.25 | convolution fusion | flops 604372992 | bytes 13443072 | tf_op jit(solution)/shard_map/dot_general | solution.py:31
  136.9 8.0 %fusion.24 = bf16[48,8192]{1,0:T(8,128)(2,1)} fusion(bf16[48,768]{1,0:T(8,128)(2,1)S(1)} %reshape.147, bf16[2,768,8192]{2,1,0:T(8,128)(2,1)} %param.11), kind=kOutput, calls=%fused_computation.24 | convolution fusion | flops 604372992 | bytes 13443072 | tf_op jit(solution)/shard_map/dot_general | solution.py:30
  145.0 13.5 %reduce-scatter.11.cloned.1.call-done = bf16[48,2048]{1,0:T(8,128)(2,1)} async-done(((bf16[48,8192]{1,0:T(8,128)(2,1)}), bf16[48,2048]{1,0:T(8,128)(2,1)}) %reduce-scatter.11.cloned.1.call-update) | async-done | bytes 196624 | tf_op jit(solution)/shard_map/reduce_scatter | solution.py:36
  158.4 25.7 %reduce-scatter.9.cloned.1.call-done = bf16[48,2048]{1,0:T(8,128)(2,1)} async-done(((bf16[48,8192]{1,0:T(8,128)(2,1)}), bf16[48,2048]{1,0:T(8,128)(2,1)}) %reduce-scatter.9.cloned.1.call-update) | async-done | bytes 196624 | tf_op jit(solution)/shard_map/reduce_scatter | solution.py:33
  184.1 1.1 fusion.44
  185.2 8.0 %all_gather.7 = bf16[48,8192]{1,0:T(8,128)(2,1)S(1)} all-gather(bf16[48,2048]{1,0:T(8,128)(2,1)S(1)} %fusion.44), channel_id=1, replica_groups=mesh['groups'=2,'expert'=4,'tensor'=4] {'tensor'}, dimensions={1}, use_global_device_ids=true | all-gather | bytes 983040 | tf_op jit(solution)/shard_map/all_gather | solution.py:42
  193.3 6.8 %fusion.33 = bf16[48,768]{1,0:T(8,128)(2,1)S(1)} fusion(bf16[48,8192]{1,0:T(8,128)(2,1)S(1)} %all_gather.7, bf16[2,8192,768]{2,1,0:T(8,128)(2,1)} %param.13), kind=kOutput, calls=%fused_computation.27 | convolution fusion | flops 604016640 | bytes 13443072 | tf_op jit(solution)/shard_map/dot_general | solution.py:41
  200.1 0.6 reshape.148
  200.7 4.6 %all-to-all-start.3 = ((bf16[4,12,768]{2,1,0:T(8,128)(2,1)}), bf16[4,12,768]{2,1,0:T(8,128)(2,1)S(1)}, u32[]{:S(2)}, u32[]{:S(2)}) async-start(bf16[4,12,768]{2,1,0:T(8,128)(2,1)} %reshape.148), calls=%async_computation.7 | async-start | bytes 196608 | tf_op jit(solution)/shard_map/all_to_all | solution.py:47
  205.3 6.0 %all-to-all-done.3 = bf16[4,12,768]{2,1,0:T(8,128)(2,1)S(1)} async-done(((bf16[4,12,768]{2,1,0:T(8,128)(2,1)}), bf16[4,12,768]{2,1,0:T(8,128)(2,1)S(1)}, u32[]{:S(2)}, u32[]{:S(2)}) %all-to-all-start.3) | async-done | bytes 73760 | tf_op jit(solution)/shard_map/all_to_all | solution.py:47
  211.3 0.6 gather_fusion.1
  212.2 0.6 fusion.53
  (55 shorter events, 3.4 us)
Async XLA Ops:
  6.5 53.4 %reduce-scatter.5.cloned.1.call-start = ((), (), s32[]{:S(2)}) async-start(), calls=%async_computation.8 | async-start | bytes 983040 | tf_op jit(solution)/shard_map/reduce_scatter | solution.py:33
  31.0 15.9 %copy-start.1 = (f32[2,2,8,2]{2,3,1,0:T(2,128)S(1)}, f32[2,2,8,2]{2,3,1,0:T(2,128)}, u32[]{:S(2)}) copy-start(f32[2,2,8,2]{2,3,1,0:T(2,128)} %param.9) | copy-start | bytes 772
  38.8 46.9 %reduce-scatter.7.cloned.1.call-start = ((), (), s32[]{:S(2)}) async-start(), calls=%async_computation.9 | async-start | bytes 983040 | tf_op jit(solution)/shard_map/reduce_scatter | solution.py:36
  46.8 67.0 %copy-start = (bf16[2,8,768]{2,1,0:T(8,128)(2,1)S(1)}, bf16[2,8,768]{2,1,0:T(8,128)(2,1)}, u32[]{:S(2)}) copy-start(bf16[2,8,768]{2,1,0:T(8,128)(2,1)} %param.7) | copy-start | bytes 73732
  102.4 10.6 %all-to-all-start.1 = ((bf16[4,12,768]{2,1,0:T(8,128)(2,1)}), bf16[4,12,768]{2,1,0:T(8,128)(2,1)S(1)}, u32[]{:S(2)}, u32[]{:S(2)}) async-start(bf16[4,12,768]{2,1,0:T(8,128)(2,1)} %reshape.143), calls=%async_computation.3 | async-start | bytes 196608 | tf_op jit(solution)/shard_map/all_to_all | solution.py:47
  107.0 51.5 %reduce-scatter.11.cloned.1.call-start = ((), (), s32[]{:S(2)}) async-start(), calls=%async_computation.11 | async-start | bytes 983040 | tf_op jit(solution)/shard_map/reduce_scatter | solution.py:36
  136.9 47.2 %reduce-scatter.9.cloned.1.call-start = ((), (), s32[]{:S(2)}) async-start(), calls=%async_computation.10 | async-start | bytes 983040 | tf_op jit(solution)/shard_map/reduce_scatter | solution.py:33
  200.7 10.6 %all-to-all-start.3 = ((bf16[4,12,768]{2,1,0:T(8,128)(2,1)}), bf16[4,12,768]{2,1,0:T(8,128)(2,1)S(1)}, u32[]{:S(2)}, u32[]{:S(2)}) async-start(bf16[4,12,768]{2,1,0:T(8,128)(2,1)} %reshape.148), calls=%async_computation.7 | async-start | bytes 196608 | tf_op jit(solution)/shard_map/all_to_all | solution.py:47
Sparse Core Ops, SparseCore 0:
  38.9 20.9 reduce-scatter.4
  62.5 23.1 reduce-scatter.6
  137.0 21.4 reduce-scatter.10
  160.8 23.2 reduce-scatter.8
where the time goes:
time: 220 us; the launch traced here: 219 us
  waiting for transfers between devices  89.9 us (41%)
  blocking collectives  49 us (22%)
  matrix products  45.1 us (20%)
  between operations  13.3 us (6%)
  starting transfers between devices  9.27 us (4%)
  other arithmetic  6.42 us (3%)
  local copies, waits for them, and re-layouts  6.24 us (3%)
    reduce_scatter x2, waiting for transfers between devices, make_expert(): lax.psum_scatter(up_part.astype(jnp.bfloat16), 'tensor', scatter_dimensio...  39.2 us
    reduce_scatter x2, waiting for transfers between devices, make_expert(): lax.psum_scatter(gate_part.astype(jnp.bfloat16), 'tensor', scatter_dimens...  38.7 us
    all_to_all x2, blocking collectives, run_layer(): lax.all_to_all(sending, 'expert', split_axis=0, concat_axis=0, tiled=True)  19 us
    all_gather x2, blocking collectives, make_expert(): lax.all_gather(hidden, 'tensor', axis=1, tiled=True)  16.1 us
    dot_general x2, matrix products, make_expert(): gate_part = jnp.dot(inputs, gate_matrix, preferred_element_type=jnp.float32)  15.8 us
    dot_general x2, matrix products, make_expert(): up_part = jnp.dot(inputs, up_matrix, preferred_element_type=jnp.float32)  15.8 us
    psum x2, blocking collectives, run_layer(): squares = lax.psum(jnp.sum(values * values, axis=2), 'tensor')  14 us
    dot_general x2, matrix products, make_expert(): jnp.dot(lax.all_gather(hidden, 'tensor', axis=1, tiled=True), down_weight...  13.6 us
  transfers between devices with their start and end apart: 6, of which 6 were waited for; matrix products, arithmetic and copies ran while one was open for 7% of the time, Pallas kernels for 0%

commit v1 on v0

v1 whole, which is shorter than its diff:
```python
import functools

import jax
import jax.numpy as jnp
from jax import lax
from jax.experimental import pallas as pl
from jax.experimental.pallas import tpu as pltpu
from jax.sharding import PartitionSpec as P

EXPERTS = 4
MESH_ID = pl.DeviceIdType.MESH
F32 = jnp.float32
BF16 = jnp.bfloat16


def reversed_bits(value, bits):
    out = 0
    for k in range(bits):
        out = out * 2 + (value >> k) % 2
    return out


def kernel(
    cfg,
    tok_ref,
    ids_ref,
    gates_ref,
    gain_ref,
    wg_ref,
    wu_ref,
    wd_ref,
    out_ref,
    wg_buf,
    wu_buf,
    wd_buf,
    x_ref,
    disp,
    arrived,
    xin,
    sqs,
    scale,
    part,
    hid,
    acc,
    back,
    ret,
    *rest,
):
    layers, micro, tok, ranks, T, width, chunks, W, wq, cap, SR = cfg
    nb = T.bit_length() - 1
    rbufs = rest[:nb]
    abufs = rest[nb : 2 * nb - 1]
    wsem, d_send, d_recv, s_send, s_recv, b_send, b_recv, rs_send, rs_recv, ag_send, ag_recv = rest[2 * nb - 1 :]
    t = lax.axis_index("tensor")
    e = lax.axis_index("expert")
    sharing = ranks // EXPERTS
    rows = micro * tok
    R = ranks * micro * cap
    feature_count = width * T
    bits = [(t // (1 << k)) % 2 for k in range(nb)]
    partner = [t + (1 - 2 * bits[k]) * (1 << k) for k in range(nb)]
    s_me = sum(bits[k] * (T >> (k + 1)) for k in range(nb))

    def wg_copy(l, c):
        return pltpu.make_async_copy(
            wg_ref.at[l, :, pl.ds(pl.multiple_of(c * W, W), W)], wg_buf.at[c], wsem.at[0, c]
        )

    def wu_copy(l, c):
        return pltpu.make_async_copy(
            wu_ref.at[l, :, pl.ds(pl.multiple_of(c * W, W), W)], wu_buf.at[c], wsem.at[1, c]
        )

    def wd_copy(l, c):
        return pltpu.make_async_copy(
            wd_ref.at[l, pl.ds(pl.multiple_of(c * W, W), W), :], wd_buf.at[c], wsem.at[2, c]
        )

    def start_gu(c, _):
        wg_copy(0, c).start()
        wu_copy(0, c).start()
        return 0

    def start_d(c, _):
        wd_copy(0, c).start()
        return 0

    lax.fori_loop(0, chunks, start_gu, 0)
    lax.fori_loop(0, chunks, start_d, 0)

    barrier = pltpu.get_barrier_semaphore()
    for d in range(1, T):
        pl.semaphore_signal(barrier, inc=1, device_id={"tensor": (t + d) % T}, device_id_type=MESH_ID)
    for d in range(1, ranks):
        pl.semaphore_signal(barrier, inc=1, device_id={"expert": (e + d) % ranks}, device_id_type=MESH_ID)

    def disp_copy(l, d):
        peer = (e + d) % ranks
        return pltpu.make_async_remote_copy(
            src_ref=disp.at[l, peer // sharing],
            dst_ref=arrived.at[l, e],
            send_sem=d_send.at[l, d],
            recv_sem=d_recv.at[l, d],
            device_id={"expert": peer},
            device_id_type=MESH_ID,
        )

    def sq_copy(l, d):
        return pltpu.make_async_remote_copy(
            src_ref=sqs.at[l, t],
            dst_ref=sqs.at[l, t],
            send_sem=s_send.at[l, d],
            recv_sem=s_recv.at[l, d],
            device_id={"tensor": (t + d) % T},
            device_id_type=MESH_ID,
        )

    def back_copy(l, d):
        peer = (e + d) % ranks
        return pltpu.make_async_remote_copy(
            src_ref=back.at[l, peer],
            dst_ref=ret.at[l, e],
            send_sem=b_send.at[l, d],
            recv_sem=b_recv.at[l, d],
            device_id={"expert": peer},
            device_id_type=MESH_ID,
        )

    def rs_copy(l, c, k):
        half = T >> (k + 1)
        source = part if k == 0 else abufs[k - 1]
        return pltpu.make_async_remote_copy(
            src_ref=source.at[l, c, pl.ds((1 - bits[k]) * half, half)],
            dst_ref=rbufs[k].at[l, c],
            send_sem=rs_send.at[k, l, c],
            recv_sem=rs_recv.at[k, l, c],
            device_id={"tensor": partner[k]},
            device_id_type=MESH_ID,
        )

    def ag_copy(l, c, k):
        size = T >> (k + 1)
        base = sum(bits[i] * (T >> (i + 1)) for i in range(k + 1))
        block = hid.at[l, c, pl.ds(base, size)]
        return pltpu.make_async_remote_copy(
            src_ref=block,
            dst_ref=block,
            send_sem=ag_send.at[k, l, c],
            recv_sem=ag_recv.at[k, l, c],
            device_id={"tensor": partner[k]},
            device_id_type=MESH_ID,
        )

    x_ref[...] = tok_ref[...].astype(F32)

    dense = lax.broadcasted_iota(jnp.int32, (R, ranks * SR), 0)
    padded = lax.broadcasted_iota(jnp.int32, (R, ranks * SR), 1)
    place = padded & (SR - 1)
    shift = SR.bit_length() - 1
    pack = jnp.where(
        (dense == (padded >> shift) * (micro * cap) + place) & (place < micro * cap), 1.0, 0.0
    ).astype(BF16)

    row_i = lax.broadcasted_iota(jnp.int32, (rows, rows), 0)
    col_i = lax.broadcasted_iota(jnp.int32, (rows, rows), 1)
    same_micro = row_i >= 0
    for j in range(1, micro):
        same_micro = same_micro & ((row_i >= j * tok) == (col_i >= j * tok))
    own_micro = jnp.zeros((rows, 1), F32)
    row_one = lax.broadcasted_iota(jnp.int32, (rows, 1), 0)
    for j in range(1, micro):
        own_micro = own_micro + jnp.where(row_one >= j * tok, 1.0, 0.0)
    slot_iota = lax.broadcasted_iota(jnp.int32, (rows, EXPERTS * SR), 1).astype(F32)

    def slot_hits(l):
        ids = ids_ref[l].astype(F32)
        cols = [ids[:, 0:1], ids[:, 1:2]]
        across = [jnp.sum(jnp.where(row_i == col_i, c, 0.0), axis=0, keepdims=True) for c in cols]
        hits = []
        for k in range(2):
            position = jnp.zeros((rows, 1), F32)
            for other in range(2):
                before = (col_i <= row_i) if other < k else (col_i < row_i)
                match = (cols[k] == across[other]) & before & same_micro
                position = position + jnp.sum(jnp.where(match, 1.0, 0.0), axis=1, keepdims=True)
            slot = cols[k] * SR + own_micro * cap + position
            hits.append(jnp.where(slot == slot_iota, 1.0, 0.0))
        return hits

    lags = [1 if (k == 0 and T == 4) else 2 for k in range(nb)]
    rs_off = [sum(lags[: k + 1]) for k in range(nb)]
    ag_off, at = [0] * nb, rs_off[-1]
    for k in reversed(range(nb)):
        at += lags[k]
        ag_off[k] = at

    def layer(l, _):
        hits = slot_hits(l)
        picks = (hits[0] + hits[1]).astype(BF16)
        out_rows = lax.dot_general(
            picks, x_ref[...].astype(BF16), (((0,), (0,)), ((), ())), preferred_element_type=F32
        )
        disp[l] = out_rows.astype(BF16).reshape(EXPERTS, SR, width)

        @pl.when(l == 0)
        def _():
            pl.semaphore_wait(barrier, T + ranks - 2)

        for d in range(1, ranks):
            disp_copy(l, d).start()
        arrived[l, e] = disp[l, e // sharing]
        for d in range(1, ranks):
            disp_copy(l, d).wait_recv()
        got = jnp.dot(
            pack, arrived[l].reshape(ranks * SR, width), preferred_element_type=F32
        )
        squares = jnp.sum(got * got, axis=1, keepdims=True)
        sqs[l, t] = jnp.broadcast_to(squares, (R, 128))
        for d in range(1, T):
            sq_copy(l, d).start()
        xin[...] = (got * gain_ref[l]).astype(BF16)
        acc[...] = jnp.zeros_like(acc)

        def gate_up(c):
            wg_copy(l, c).wait()
            wu_copy(l, c).wait()
            for q in range(T):
                s = reversed_bits(q, nb)
                part[l, c, s, :, 0:wq] = jnp.dot(
                    xin[...], wg_buf[c, :, q * wq : (q + 1) * wq], preferred_element_type=F32
                ).astype(BF16)
                part[l, c, s, :, wq : 2 * wq] = jnp.dot(
                    xin[...], wu_buf[c, :, q * wq : (q + 1) * wq], preferred_element_type=F32
                ).astype(BF16)
            rs_copy(l, c, 0).start()

            @pl.when(l + 1 < layers)
            def _():
                wg_copy(l + 1, c).start()
                wu_copy(l + 1, c).start()

        def reduce(c, k):
            half = T >> (k + 1)
            rs_copy(l, c, k).wait_recv()
            source = part if k == 0 else abufs[k - 1]
            total = source[l, c, pl.ds(bits[k] * half, half)].astype(F32) + rbufs[k][l, c].astype(F32)
            if k < nb - 1:
                abufs[k][l, c] = total.astype(BF16)
                rs_copy(l, c, k + 1).start()
            else:
                factor = scale[:, 0:1]
                gate = total[0, :, 0:wq] * factor
                up = total[0, :, wq : 2 * wq] * factor
                hid[l, c, s_me] = (gate / (1.0 + jnp.exp(-gate)) * up).astype(BF16)
                ag_copy(l, c, nb - 1).start()

        def gather(c, k):
            ag_copy(l, c, k).wait_recv()
            if k > 0:
                ag_copy(l, c, k - 1).start()
            else:
                down(c)

        def down(c):
            wd_copy(l, c).wait()
            total = acc[...]
            for s in range(T):
                q = reversed_bits(s, nb)
                total = total + jnp.dot(
                    hid[l, c, s], wd_buf[c, q * wq : (q + 1) * wq, :], preferred_element_type=F32
                )
            acc[...] = total

            @pl.when(l + 1 < layers)
            def _():
                wd_copy(l + 1, c).start()

        def step(i, _):
            @pl.when(i < chunks)
            def _():
                gate_up(i)

            @pl.when(i == rs_off[-1])
            def _():
                for d in range(1, T):
                    sq_copy(l, d).wait_recv()
                total = sqs[l, 0]
                for j in range(1, T):
                    total = total + sqs[l, j]
                scale[...] = lax.rsqrt(total / feature_count + 1e-05)

            for k in range(nb):
                c = i - rs_off[k]
                pl.when((c >= 0) & (c < chunks))(functools.partial(reduce, c, k))
            for k in reversed(range(nb)):
                c = i - ag_off[k]
                pl.when((c >= 0) & (c < chunks))(functools.partial(gather, c, k))
            return 0

        lax.fori_loop(0, chunks + ag_off[0], step, 0)

        spread = lax.dot_general(
            pack, acc[...].astype(BF16), (((0,), (0,)), ((), ())), preferred_element_type=F32
        )
        back[l] = spread.astype(BF16).reshape(ranks, SR, width)
        for d in range(1, ranks):
            back_copy(l, d).start()
        ret[l, e] = back[l, e]
        gates = gates_ref[l]
        weights = hits[0] * gates[:, 0:1] + hits[1] * gates[:, 1:2]
        for d in range(1, ranks):
            back_copy(l, d).wait_recv()
        results = ret[l].astype(F32)
        if sharing > 1:
            results = jnp.sum(results.reshape(EXPERTS, sharing, SR, width), axis=1)
        mixture = jnp.dot(
            weights,
            results.reshape(EXPERTS * SR, width),
            preferred_element_type=F32,
            precision=lax.Precision.HIGHEST,
        )
        x_ref[...] = (x_ref[...] + mixture).astype(BF16).astype(F32)
        return 0

    lax.fori_loop(0, layers, layer, 0)
    out_ref[...] = x_ref[...].astype(BF16)

    def drain(l, _):
        for d in range(1, ranks):
            disp_copy(l, d).wait_send()
            back_copy(l, d).wait_send()
        for d in range(1, T):
            sq_copy(l, d).wait_send()

        def drain_chunk(c, _):
            for k in range(nb):
                rs_copy(l, c, k).wait_send()
                ag_copy(l, c, k).wait_send()
            return 0

        lax.fori_loop(0, chunks, drain_chunk, 0)
        return 0

    lax.fori_loop(0, layers, drain, 0)


def shards(ranks, T, tokens, route_ids, route_gates, norm_gain, gate_weights, up_weights, down_weights):
    micro, tok, width = tokens.shape
    layers = route_ids.shape[0]
    hidden = gate_weights.shape[2]
    rows = micro * tok
    cap = 3 * tok // 4
    SR = 16
    while SR < micro * cap:
        SR *= 2
    chunks = 8
    while chunks > 1 and hidden // chunks < 256 * T:
        chunks //= 2
    W = hidden // chunks
    wq = W // T
    nb = T.bit_length() - 1
    R = ranks * micro * cap
    cfg = (layers, micro, tok, ranks, T, width, chunks, W, wq, cap, SR)
    vmem = pl.BlockSpec(memory_space=pltpu.VMEM)
    hbm = pl.BlockSpec(memory_space=pl.ANY)
    dma = pltpu.SemaphoreType.DMA
    out = pl.pallas_call(
        functools.partial(kernel, cfg),
        out_shape=jax.ShapeDtypeStruct((rows, width), BF16),
        in_specs=[vmem] * 4 + [hbm] * 3,
        out_specs=vmem,
        scratch_shapes=[
            pltpu.VMEM((chunks, width, W), BF16),
            pltpu.VMEM((chunks, width, W), BF16),
            pltpu.VMEM((chunks, W, width), BF16),
            pltpu.VMEM((rows, width), F32),
            pltpu.VMEM((layers, EXPERTS, SR, width), BF16),
            pltpu.VMEM((layers, ranks, SR, width), BF16),
            pltpu.VMEM((R, width), BF16),
            pltpu.VMEM((layers, T, R, 128), F32),
            pltpu.VMEM((R, 128), F32),
            pltpu.VMEM((layers, chunks, T, R, 2 * wq), BF16),
            pltpu.VMEM((layers, chunks, T, R, wq), BF16),
            pltpu.VMEM((R, width), F32),
            pltpu.VMEM((layers, ranks, SR, width), BF16),
            pltpu.VMEM((layers, ranks, SR, width), BF16),
        ]
        + [pltpu.VMEM((layers, chunks, T >> (k + 1), R, 2 * wq), BF16) for k in range(nb)]
        + [pltpu.VMEM((layers, chunks, T >> (k + 1), R, 2 * wq), BF16) for k in range(nb - 1)]
        + [
            dma((3, chunks)),
            dma((layers, ranks)),
            dma((layers, ranks)),
            dma((layers, T)),
            dma((layers, T)),
            dma((layers, ranks)),
            dma((layers, ranks)),
            dma((nb, layers, chunks)),
            dma((nb, layers, chunks)),
            dma((nb, layers, chunks)),
            dma((nb, layers, chunks)),
        ],
        compiler_params=pltpu.CompilerParams(
            collective_id=0, has_side_effects=True, vmem_limit_bytes=64 * 1024 * 1024 - 65536
        ),
    )(
        tokens.reshape(rows, width),
        route_ids.reshape(layers, rows, 2),
        route_gates.reshape(layers, rows, 2),
        norm_gain.reshape(layers, 1, width),
        gate_weights,
        up_weights,
        down_weights,
    )
    return out.reshape(micro, tok, width)


def solution(mesh):
    in_specs = (
        P(None, ("groups", "expert"), "tensor"),
        P(None, None, ("groups", "expert"), None),
        P(None, None, ("groups", "expert"), None),
        P(None, "tensor"),
        P(None, "tensor", "expert"),
        P(None, "tensor", "expert"),
        P(None, "expert", "tensor"),
    )
    out_specs = P(None, ("groups", "expert"), "tensor")
    body = functools.partial(shards, mesh.shape["expert"], mesh.shape["tensor"])
    return jax.shard_map(body, mesh=mesh, in_specs=in_specs, out_specs=out_specs, check_vma=False)
```

time: 220 us -> 72 us (0.33)
  waiting for transfers between devices: 89.9 us -> 0 us
  Pallas kernels: 0 us -> 66.2 us
  blocking collectives: 49 us -> 0 us
  matrix products: 45.1 us -> 0 us
  between operations: 13.3 us -> 0.01 us
  starting transfers between devices: 9.27 us -> 0 us
  other arithmetic: 6.42 us -> 0 us
    reduce_scatter x4 -> x0, waiting for transfers between devices: 77.9 us -> none  [the longest x2 39.2 us: make_expert(): lax.psum_scatter(up_part.astype(jnp.bfloat16), 'tensor', scatter_dimensio...]
    pallas_call x0 -> x1, Pallas kernels: none -> 66.2 us  [shards(): pl.pallas_call(functools.partial(kernel, cfg), out_shape=jax.ShapeDtypeSt...]
    dot_general x6 -> x0, matrix products: 45.1 us -> none  [the longest x2 15.8 us: make_expert(): gate_part = jnp.dot(inputs, gate_matrix, preferred_element_type=jnp.float32)]
    all_to_all x2 -> x0, blocking collectives: 19 us -> none  [run_layer(): lax.all_to_all(sending, 'expert', split_axis=0, concat_axis=0, tiled=True)]
    all_gather x2 -> x0, blocking collectives: 16.1 us -> none  [make_expert(): lax.all_gather(hidden, 'tensor', axis=1, tiled=True)]
    psum x2 -> x0, blocking collectives: 14 us -> none  [run_layer(): squares = lax.psum(jnp.sum(values * values, axis=2), 'tensor')]
    all_to_all x2 -> x0, waiting for transfers between devices: 12 us -> none  [make_expert(): lax.all_to_all(outgoing, 'expert', split_axis=0, concat_axis=0, tiled=True)]
    all_to_all x2 -> x0, starting transfers between devices: 9.18 us -> none  [make_expert(): lax.all_to_all(outgoing, 'expert', split_axis=0, concat_axis=0, tiled=True)]
  transfers between devices with their start and end apart: 6 -> 0, of which waited for: 6 -> 0; matrix products, arithmetic and copies ran while one was open for 7% -> 0% of each run, Pallas kernels for 0% -> 0%
where the time goes in v1:
time: 72 us; the launch traced here: 71.6 us
  Pallas kernels  66.2 us (92%)
  local copies, waits for them, and re-layouts  5.39 us (7%)
    pallas_call x1, Pallas kernels, shards(): pl.pallas_call(functools.partial(kernel, cfg), out_shape=jax.ShapeDtypeSt...  66.2 us

profile of v1, /device:TPU:0, one launch (start us, length us, event | category | flops | bytes accessed | tf_op | source)
XLA Modules:
  0.0 71.6 jit_solution(11021630782887573883)
XLA Ops:
  0.0 1.3 %reshape.18.gain_ref = f32[2,1,768]{2,1,0:T(1,128)} reshape(f32[2,768]{1,0:T(2,128)} %param.10) | data formatting | bytes 12288 | tf_op jit(solution)/shard_map/reshape | solution.py:410
  1.3 1.4 %copy.12 = s32[2,2,8,2]{3,2,1,0:T(8,128)} copy(s32[2,2,8,2]{2,3,1,0:T(2,128)} %param.8) | data formatting | bytes 512 | tf_op jit(solution)/shard_map/reshape | solution.py:408
  2.7 1.4 %copy.13 = f32[2,2,8,2]{3,2,1,0:T(8,128)} copy(f32[2,2,8,2]{2,3,1,0:T(2,128)} %param.9) | data formatting | bytes 512 | tf_op jit(solution)/shard_map/reshape | solution.py:409
  4.0 66.2 %shard_map.73 = bf16[16,768]{1,0:T(8,128)(2,1)} custom-call(bf16[16,768]{1,0:T(8,128)(2,1)} %bitcast.7, s32[2,16,2]{2,1,0:T(8,128)} %bitcast.5, f32[2,16,2]{2,1,0:T(8,128)} %bitcast.6, f32[2,1,768]{2,1,0:T(1,128)} %reshape.18.gain_ref, bf16[2,768,8192]{2,1,0:T(8,128)(2,1)} %wg_ref.1, bf16[2,768,8192]{2,1,0:T(8,128)(2,1)} %wu_ref.1, bf16[2,8192,768]{2,1,0:T(8,128)(2,1)} %wd_ref.1), custom_call_target="tpu_custom_call" | custom-call | tf_op jit(solution)/shard_map/pallas_call | solution.py:367
  70.3 1.3 %copy.17 = bf16[2,8,768]{2,1,0:T(8,128)(2,1)} copy(bf16[2,8,768]{2,1,0:T(8,128)(2,1)} %bitcast.4) | data formatting | bytes 49152

commit v2 on v1

--- a/solution.py
+++ b/solution.py
@@ -187,7 +187,7 @@
             hits.append(jnp.where(slot == slot_iota, 1.0, 0.0))
         return hits
 
-    lags = [1 if (k == 0 and T == 4) else 2 for k in range(nb)]
+    lags = [1 if (k == 0 and T == 4) else 3 for k in range(nb)]
     rs_off = [sum(lags[: k + 1]) for k in range(nb)]
     ag_off, at = [0] * nb, rs_off[-1]
     for k in reversed(range(nb)):

time: 72 us -> 69.9 us (0.971)
  Pallas kernels: 66.2 us -> 64.2 us
    pallas_call x1, Pallas kernels: 66.2 us -> 64.2 us  [shards(): pl.pallas_call(functools.partial(kernel, cfg), out_shape=jax.ShapeDtypeSt...]
where the time goes in v2:
time: 69.9 us; the launch traced here: 69.6 us
  Pallas kernels  64.2 us (92%)
  local copies, waits for them, and re-layouts  5.39 us (8%)
    pallas_call x1, Pallas kernels, shards(): pl.pallas_call(functools.partial(kernel, cfg), out_shape=jax.ShapeDtypeSt...  64.2 us

profile of v2, /device:TPU:0, one launch (start us, length us, event | category | flops | bytes accessed | tf_op | source)
XLA Modules:
  0.0 69.6 jit_solution(1969893527900177264)
XLA Ops:
  0.0 1.3 %reshape.18.gain_ref = f32[2,1,768]{2,1,0:T(1,128)} reshape(f32[2,768]{1,0:T(2,128)} %param.10) | data formatting | bytes 12288 | tf_op jit(solution)/shard_map/reshape | solution.py:410
  1.3 1.4 %copy.12 = s32[2,2,8,2]{3,2,1,0:T(8,128)} copy(s32[2,2,8,2]{2,3,1,0:T(2,128)} %param.8) | data formatting | bytes 512 | tf_op jit(solution)/shard_map/reshape | solution.py:408
  2.7 1.4 %copy.13 = f32[2,2,8,2]{3,2,1,0:T(8,128)} copy(f32[2,2,8,2]{2,3,1,0:T(2,128)} %param.9) | data formatting | bytes 512 | tf_op jit(solution)/shard_map/reshape | solution.py:409
  4.0 64.2 %shard_map.73 = bf16[16,768]{1,0:T(8,128)(2,1)} custom-call(bf16[16,768]{1,0:T(8,128)(2,1)} %bitcast.7, s32[2,16,2]{2,1,0:T(8,128)} %bitcast.5, f32[2,16,2]{2,1,0:T(8,128)} %bitcast.6, f32[2,1,768]{2,1,0:T(1,128)} %reshape.18.gain_ref, bf16[2,768,8192]{2,1,0:T(8,128)(2,1)} %wg_ref.1, bf16[2,768,8192]{2,1,0:T(8,128)(2,1)} %wu_ref.1, bf16[2,8192,768]{2,1,0:T(8,128)(2,1)} %wd_ref.1), custom_call_target="tpu_custom_call" | custom-call | tf_op jit(solution)/shard_map/pallas_call | solution.py:367
  68.2 1.3 %copy.17 = bf16[2,8,768]{2,1,0:T(8,128)(2,1)} copy(bf16[2,8,768]{2,1,0:T(8,128)(2,1)} %bitcast.4) | data formatting | bytes 49152
